TPU v7x, 32 devices: a whole 2x2x4 slice. The times are simulated.
32 devices in a mesh: layer: 2 (over core), row: 4 (over y, x), col: 4 (over z).
Axes of the slice: x: 2, y: 2, z: 4, core: 2. Of those that a mesh axis runs over, the one named last changes fastest.
Arguments:
- left_matrix: bfloat16 [2048, 16384], P('row', ('layer', 'col')), may hold values from -6 to 6
- right_matrix: bfloat16 [16384, 8192], P(('layer', 'row'), 'col'), may hold values from -0.046875 to 0.046875
Outputs:
- product: bfloat16 [2048, 8192], P(('row', 'layer'), 'col')
All inputs are finite; a program needn't handle non-finite values.
Results may differ from a plain program's by a relative error of at most 0.001.
Values may be sent and summed in bfloat16 or wider, within the bound.
A program may use at most 128 MiB of HBM per device.

v0:
```python
import functools

import jax
import jax.numpy as jnp
from jax import lax
from jax.experimental import pallas as pl
from jax.experimental.pallas import tpu as pltpu
from jax.sharding import PartitionSpec as P

MESH = pl.DeviceIdType.MESH
CHUNKS = 8
STRIPS = 8
LATE = 5


def kernel(R, NC, NB, a_hbm, b_hbm, o_hbm, zbuf, pbuf, bown, bin_, cbuf, xbuf, rbuf, obuf,
           la, lb, zs, zr, ps, pr, bs, br, ds, dr, cs, cr, lo):
    l = lax.axis_index("layer")
    i = lax.axis_index("row")
    z = lax.axis_index("col")
    x = lax.rem(i, 2)
    y = lax.div(i, 2)
    xn = 2 * y + 1 - x
    yn = 2 * (1 - y) + x
    rows = zbuf.shape[1]
    CH = rows // NC
    half = rows // 2
    W = bown.shape[2]

    def chunk(c):
        return pl.ds(pl.multiple_of(c * CH, CH), CH)

    def a_copy(c):
        return pltpu.make_async_copy(a_hbm.at[chunk(c)], zbuf.at[z, chunk(c)], la.at[c])

    def b_copy(n):
        return pltpu.make_async_copy(b_hbm.at[:, pl.ds(n * W, W)], bown.at[n], lb.at[n])

    def remote(src, dst, send, recv, **where):
        return pltpu.make_async_remote_copy(
            src_ref=src, dst_ref=dst, send_sem=send, recv_sem=recv,
            device_id=where, device_id_type=MESH)

    def z_send(d, k, c):
        sign = 1 - 2 * d
        zb = z - sign * k
        return remote(zbuf.at[zb, chunk(c)], zbuf.at[zb, chunk(c)], zs.at[d, k, c], zr.at[d, k, c], col=z + sign)

    def z_recv(d, k, c):
        sign = 1 - 2 * d
        zb = z - sign * k
        return remote(zbuf.at[zb, chunk(c)], zbuf.at[zb, chunk(c)], zs.at[d, k - 1, c], zr.at[d, k - 1, c], col=z - sign)

    def p_send(zb, c):
        v = lax.div(zb, 2)
        return remote(zbuf.at[zb, chunk(c)], pbuf.at[v, chunk(c)], ps.at[v, c], pr.at[v, c], row=xn)

    def b_send(n):
        return remote(bown.at[n], bin_.at[n], bs.at[n], br.at[n], row=yn)

    def d_send(n):
        return remote(cbuf.at[n, 1 - l], xbuf.at[n], ds.at[n], dr.at[n], layer=1 - l)

    def c_send(n):
        return remote(cbuf.at[n, l, 1], rbuf.at[n], cs.at[n], cr.at[n], row=xn)

    for c in range(NC):
        a_copy(c).start()
    for n in range(NB):
        b_copy(n).start()

    barrier = pltpu.get_barrier_semaphore()
    pl.semaphore_signal(barrier, inc=1, device_id={"row": xn}, device_id_type=MESH)
    pl.semaphore_signal(barrier, inc=1, device_id={"row": yn}, device_id_type=MESH)
    pl.semaphore_signal(barrier, inc=1, device_id={"layer": 1 - l}, device_id_type=MESH)

    @pl.when(z > 0)
    def _():
        pl.semaphore_signal(barrier, inc=1, device_id={"col": z - 1}, device_id_type=MESH)

    @pl.when(z < R - 1)
    def _():
        pl.semaphore_signal(barrier, inc=1, device_id={"col": z + 1}, device_id_type=MESH)

    pl.semaphore_wait(barrier, 3 + (z > 0).astype(jnp.int32) + (z < R - 1).astype(jnp.int32))

    def outward(k, c, act):
        for d in range(2):
            sign = 1 - 2 * d
            zb = z - sign * k
            nxt = z + sign

            @pl.when((zb >= 0) & (zb < R) & (nxt >= 0) & (nxt < R))
            def _():
                act(z_send(d, k, c))

    @pl.loop(0, NC)
    def _(c):
        a_copy(c).wait()
        outward(0, c, lambda s: s.start())

        @pl.when(lax.rem(z, 2) != x)
        def _():
            p_send(z, c).start()

    @pl.loop(0, NB)
    def _(n):
        b_copy(n).wait()
        b_send(n).start()

    @pl.loop(0, (R - 1) * NC)
    def _(s):
        k = lax.div(s, NC) + 1
        c = lax.rem(s, NC)
        for d in range(2):
            sign = 1 - 2 * d
            zb = z - sign * k
            nxt = z + sign

            @pl.when((zb >= 0) & (zb < R))
            def _():
                z_recv(d, k, c).wait_recv()

                @pl.when((nxt >= 0) & (nxt < R))
                def _():
                    z_send(d, k, c).start()

                @pl.when(lax.rem(zb + R, 2) != x)
                def _():
                    p_send(zb, c).start()

    @pl.loop(0, NC)
    def _(c):
        for v in range(R // 2):
            remote(pbuf.at[v, chunk(c)], pbuf.at[v, chunk(c)], pr.at[v, c], pr.at[v, c], row=xn).wait_recv()

    def settle(n):
        d_send(n).wait_recv()
        cbuf[n, l, 1] = cbuf[n, l, 1] + xbuf[n, 1]
        c_send(n).start()
        cbuf[n, l, 0] = cbuf[n, l, 0] + xbuf[n, 0]

    def finish(n):
        c_send(n).wait_recv()
        obuf[n] = (cbuf[n, l, 0] + rbuf[n]).astype(jnp.bfloat16)
        pltpu.make_async_copy(obuf.at[n], o_hbm.at[:, pl.ds(n * W, W)], lo.at[n]).start()

    def multiply(n):
        b_send(n).wait_recv()
        for s, left in ((1, pbuf), (0, zbuf)):
            near, far = (y, 1 - y) if s else (2 * y + x, 2 * (1 - y) + x)
            for h in range(2):
                part = pl.ds(h * half, half)
                cbuf[n, h, s] = (
                    jnp.dot(left[near, part], bown[n], preferred_element_type=jnp.float32)
                    + jnp.dot(left[far, part], bin_[n], preferred_element_type=jnp.float32))
        d_send(n).start()

    @pl.loop(0, NB)
    def _(n):
        multiply(n)

        @pl.when((n > 0) & (n <= LATE))
        def _():
            settle(n - 1)

        @pl.when(n >= LATE)
        def _():
            settle(n)

    @pl.loop(0, NB)
    def _(n):
        finish(n)

    @pl.loop(0, NC)
    def _(c):
        for k in range(R):
            outward(k, c, lambda s: s.wait_send())
        for v in range(R // 2):
            p_send(2 * v + 1 - x, c).wait_send()

    @pl.loop(0, NB)
    def _(n):
        b_send(n).wait_send()
        d_send(n).wait_send()
        c_send(n).wait_send()
        pltpu.make_async_copy(obuf.at[n], o_hbm.at[:, pl.ds(n * W, W)], lo.at[n]).wait()


def plain(left_matrix, right_matrix):
    left_rows = lax.all_gather(left_matrix, "col", axis=1, tiled=True)
    right_joined = lax.all_gather(right_matrix, "row", axis=0, tiled=True)
    summed = lax.psum_scatter(
        jnp.dot(left_rows, right_joined, preferred_element_type=jnp.float32),
        "layer",
        scatter_dimension=0,
        tiled=True,
    )
    return summed.astype(jnp.bfloat16)


def fused(R, left_matrix, right_matrix):
    rows, K = left_matrix.shape
    N = right_matrix.shape[1]
    NC, NB = CHUNKS, STRIPS
    W, half = N // NB, rows // 2
    bf16, f32 = jnp.bfloat16, jnp.float32
    dma = pltpu.SemaphoreType.DMA
    return pl.pallas_call(
        functools.partial(kernel, R, NC, NB),
        out_shape=jax.ShapeDtypeStruct((half, N), bf16),
        in_specs=[pl.BlockSpec(memory_space=pl.ANY)] * 2,
        out_specs=pl.BlockSpec(memory_space=pl.ANY),
        scratch_shapes=[
            pltpu.VMEM((R, rows, K), bf16),
            pltpu.VMEM((R // 2, rows, K), bf16),
            pltpu.VMEM((NB, K, W), bf16),
            pltpu.VMEM((NB, K, W), bf16),
            pltpu.VMEM((NB, 2, 2, half, W), f32),
            pltpu.VMEM((NB, 2, half, W), f32),
            pltpu.VMEM((NB, half, W), f32),
            pltpu.VMEM((NB, half, W), bf16),
            dma((NC,)), dma((NB,)),
            dma((2, R, NC)), dma((2, R, NC)),
            dma((R // 2, NC)), dma((R // 2, NC)),
            dma((NB,)), dma((NB,)),
            dma((NB,)), dma((NB,)),
            dma((NB,)), dma((NB,)),
            dma((NB,)),
        ],
        compiler_params=pltpu.CompilerParams(
            collective_id=0, has_side_effects=True, vmem_limit_bytes=67043328),
    )(left_matrix, right_matrix)


def solution(mesh):
    shape = mesh.shape
    fits = shape["layer"] == 2 and shape["row"] == shape["col"] == 4
    local = functools.partial(fused, shape["row"]) if fits else plain
    in_specs = (P("row", ("layer", "col")), P(("layer", "row"), "col"))
    out_specs = P(("row", "layer"), "col")
    return jax.shard_map(local, mesh=mesh, in_specs=in_specs, out_specs=out_specs, check_vma=False)
```

profile of v0, /device:TPU:0, one launch (start us, length us, event | category | flops | bytes accessed | tf_op | source)
XLA Modules:
  0.0 203.4 jit_solution(9895446177209558766)
XLA Ops:
  0.0 201.1 %shard_map.28 = bf16[256,2048]{1,0:T(8,128)(2,1)} custom-call(bf16[512,2048]{1,0:T(8,128)(2,1)} %a_hbm.1, bf16[2048,2048]{1,0:T(8,128)(2,1)} %b_hbm.1), custom_call_target="tpu_custom_call" | custom-call | tf_op jit(solution)/shard_map/pallas_call | solution.py:209
  201.1 2.3 %copy.4 = bf16[256,2048]{1,0:T(8,128)(2,1)} copy(bf16[256,2048]{1,0:T(8,128)(2,1)} %shard_map.28) | data formatting | bytes 2097152
where the time goes:
time: 204 us; the launch traced here: 203 us
  Pallas kernels  201 us (99%)
  local copies, waits for them, and re-layouts  2.3 us (1%)
    pallas_call x1, Pallas kernels, fused(): pl.pallas_call(functools.partial(kernel, R, NC, NB), out_shape=jax.ShapeD...  201 us

commit v1 on v0

v1 whole, which is shorter than its diff:
```python
import functools

import jax
import jax.numpy as jnp
from jax import lax
from jax.experimental import pallas as pl
from jax.experimental.pallas import tpu as pltpu
from jax.sharding import PartitionSpec as P

MESH = pl.DeviceIdType.MESH
CHUNK_ROWS = 16
TILE = 256
PIECES = 4


def kernel(R, NC, RB, TN, NP, a_hbm, b_hbm, o_hbm, abuf, tbuf, bbuf, cbuf, dxin, dyin, sxin, syin, obuf,
           la, ls, lr, lb, bs, br, ar, us, ws, tr, tz, tx, cd, dxr, dyr, cx, cy, sxr, syr, lo):
    l = lax.axis_index("layer")
    i = lax.axis_index("row")
    z = lax.axis_index("col")
    x = lax.rem(i, 2)
    y = lax.div(i, 2)
    xn = 2 * y + 1 - x
    yn = 2 * (1 - y) + x
    dn = 2 * (1 - y) + 1 - x
    half = NC * RB
    last = R - 1
    home = i == z
    KP = bbuf.shape[1] // NP

    def remote(src, dst, send, recv, **where):
        return pltpu.make_async_remote_copy(
            src_ref=src, dst_ref=dst, send_sem=send, recv_sem=recv,
            device_id=where, device_id_type=MESH)

    def rows(m):
        return pl.ds(m * RB if isinstance(m, int) else pl.multiple_of(m * RB, RB), RB)

    def ablock(c, m):
        return abuf.at[c, :, rows(m)]

    def own(c, act_local, act_remote):
        mine = a_hbm.at[pl.ds(pl.multiple_of(l * half + c * RB, RB), RB)]
        other = a_hbm.at[pl.ds(pl.multiple_of((1 - l) * half + c * RB, RB), RB)]

        @pl.when(home)
        def _():
            spot = abuf.at[c, l, rows(i)]
            if act_local is not None:
                act_local(pltpu.make_async_copy(mine, spot, la.at[c]))
            if act_remote is not None:
                act_remote(remote(other, spot, ls.at[c], lr.at[c], layer=1 - l))

        @pl.when(jnp.logical_not(home))
        def _():
            spot = tbuf.at[c, z, l]
            if act_local is not None:
                act_local(pltpu.make_async_copy(mine, spot, la.at[c]))
            if act_remote is not None:
                act_remote(remote(other, spot, ls.at[c], lr.at[c], layer=1 - l))

    def b_rows(p):
        return pl.ds(p * KP, KP)

    def b_load(p):
        return pltpu.make_async_copy(b_hbm.at[b_rows(p)], bbuf.at[l, b_rows(p)], lb.at[p])

    def b_swap(p):
        return remote(b_hbm.at[b_rows(p)], bbuf.at[l, b_rows(p)], bs.at[p], br.at[p], layer=1 - l)

    def cross(c, k):
        return remote(tbuf.at[c, k], ablock(c, i), tx.at[c, k], ar.at[c, i], row=k)

    def ride(c, k, step):
        return remote(tbuf.at[c, k], tbuf.at[c, k], tz.at[c, k], tr.at[c, k], col=z + step)

    def transit(c, k, act):
        act(cross(c, k))

        @pl.when((i == last) & (z < last))
        def _():
            act(ride(c, k, 1))

        @pl.when((i == 0) & (z > 0))
        def _():
            act(ride(c, k, -1))

    def passing(c, act):
        for d in range(1, R):
            for side, step in ((last, -1), (0, 1)):
                k = z + step * d

                @pl.when((i == side) & (k >= 0) & (k < R))
                def _():
                    act(c, k)

    def pass_on(c, k):
        ride(c, k, 0).wait_recv()
        transit(c, k, lambda s: s.start())

    def forward(c, m, act):
        if m < last:
            @pl.when((i <= z) & (z < last))
            def _():
                act(remote(ablock(c, m), ablock(c, m), us.at[c, m], ar.at[c, m], col=z + 1))
        if m > 0:
            @pl.when((i >= z) & (z > 0))
            def _():
                act(remote(ablock(c, m), ablock(c, m), ws.at[c, m], ar.at[c, m], col=z - 1))

    def x_first(r):
        return (r == 1) | (r == 2) | ((r == 0) & (z == 2)) | ((r == 3) & (z == 1))

    here_x = x_first(i)
    side_x = x_first(xn)
    side_y = jnp.logical_not(x_first(yn))

    def far(c, act):
        @pl.when(here_x)
        def _():
            act(remote(cbuf.at[c, rows(dn)], dxin.at[c], cd.at[c], dxr.at[c], row=xn))

        @pl.when(jnp.logical_not(here_x))
        def _():
            act(remote(cbuf.at[c, rows(dn)], dyin.at[c], cd.at[c], dyr.at[c], row=yn))

    def to_x(c):
        return remote(cbuf.at[c, rows(xn)], sxin.at[c], cx.at[c], sxr.at[c], row=xn)

    def to_y(c):
        return remote(cbuf.at[c, rows(yn)], syin.at[c], cy.at[c], syr.at[c], row=yn)

    def out(c):
        return pltpu.make_async_copy(
            obuf.at[c], o_hbm.at[pl.ds(pl.multiple_of(c * RB, RB), RB)], lo.at[c])

    @pl.loop(0, NC)
    def _(c):
        own(c, lambda s: s.start(), None)

    for p in range(NP):
        b_load(p).start()

    barrier = pltpu.get_barrier_semaphore()
    for where in ({"layer": 1 - l}, {"row": xn}, {"row": yn}, {"row": dn}):
        pl.semaphore_signal(barrier, inc=1, device_id=where, device_id_type=MESH)

    @pl.when(z > 0)
    def _():
        pl.semaphore_signal(barrier, inc=1, device_id={"col": z - 1}, device_id_type=MESH)

    @pl.when(z < last)
    def _():
        pl.semaphore_signal(barrier, inc=1, device_id={"col": z + 1}, device_id_type=MESH)

    pl.semaphore_wait(barrier, 4 + (z > 0).astype(jnp.int32) + (z < last).astype(jnp.int32))

    @pl.loop(0, NC)
    def _(c):
        own(c, None, lambda s: s.start())

    for p in range(NP):
        b_swap(p).start()

    def spread(c):
        own(c, lambda s: s.wait(), lambda s: s.wait_recv())

        @pl.when(jnp.logical_not(home))
        def _():
            transit(c, z, lambda s: s.start())

        passing(c, pass_on)
        for m in range(R):
            @pl.when(jnp.logical_not(home & (i == m)))
            def _():
                remote(ablock(c, m), ablock(c, m), us.at[c, m], ar.at[c, m], col=z).wait_recv()

            forward(c, m, lambda s: s.start())

    def multiply(c):
        @pl.loop(0, bbuf.shape[2] // TN)
        def _(n):
            part = pl.ds(pl.multiple_of(n * TN, TN), TN)
            cbuf[c, :, part] = (
                jnp.dot(abuf[c, 0], bbuf[0, :, part], preferred_element_type=jnp.float32)
                + jnp.dot(abuf[c, 1], bbuf[1, :, part], preferred_element_type=jnp.float32))
        far(c, lambda s: s.start())

    def settle(c):
        @pl.when(side_y)
        def _():
            remote(dyin.at[c], dyin.at[c], cd.at[c], dyr.at[c], row=yn).wait_recv()
            cbuf[c, rows(xn)] = cbuf[c, rows(xn)] + dyin[c]
        to_x(c).start()

        @pl.when(side_x)
        def _():
            remote(dxin.at[c], dxin.at[c], cd.at[c], dxr.at[c], row=xn).wait_recv()
            cbuf[c, rows(yn)] = cbuf[c, rows(yn)] + dxin[c]
        to_y(c).start()

    def finish(c):
        to_x(c).wait_recv()
        to_y(c).wait_recv()
        obuf[c] = (cbuf[c, rows(i)] + sxin[c] + syin[c]).astype(jnp.bfloat16)
        out(c).start()

    @pl.loop(0, NC + 2)
    def _(s):
        @pl.when(s < NC)
        def _():
            spread(s)

        @pl.when(s == 0)
        def _():
            for p in range(NP):
                b_load(p).wait()
                b_swap(p).wait_recv()

        @pl.when(s < NC)
        def _():
            multiply(s)

        @pl.when((s >= 1) & (s <= NC))
        def _():
            settle(s - 1)

        @pl.when(s >= 2)
        def _():
            finish(s - 2)

    @pl.loop(0, NC)
    def _(c):
        own(c, None, lambda s: s.wait_send())

        @pl.when(jnp.logical_not(home))
        def _():
            transit(c, z, lambda s: s.wait_send())

        passing(c, lambda c, k: transit(c, k, lambda s: s.wait_send()))
        for m in range(R):
            forward(c, m, lambda s: s.wait_send())
        far(c, lambda s: s.wait_send())
        to_x(c).wait_send()
        to_y(c).wait_send()
        out(c).wait()

    for p in range(NP):
        b_swap(p).wait_send()


def plain(left_matrix, right_matrix):
    left_rows = lax.all_gather(left_matrix, "col", axis=1, tiled=True)
    right_joined = lax.all_gather(right_matrix, "row", axis=0, tiled=True)
    summed = lax.psum_scatter(
        jnp.dot(left_rows, right_joined, preferred_element_type=jnp.float32),
        "layer",
        scatter_dimension=0,
        tiled=True,
    )
    return summed.astype(jnp.bfloat16)


def fused(R, left_matrix, right_matrix):
    rows, K = left_matrix.shape
    N = right_matrix.shape[1]
    half, RB = rows // 2, CHUNK_ROWS
    NC, NP = half // RB, PIECES
    bf16, f32 = jnp.bfloat16, jnp.float32
    dma = pltpu.SemaphoreType.DMA
    return pl.pallas_call(
        functools.partial(kernel, R, NC, RB, TILE, NP),
        out_shape=jax.ShapeDtypeStruct((half, N), bf16),
        in_specs=[pl.BlockSpec(memory_space=pl.ANY)] * 2,
        out_specs=pl.BlockSpec(memory_space=pl.ANY),
        scratch_shapes=[
            pltpu.VMEM((NC, 2, R * RB, K), bf16),
            pltpu.VMEM((NC, R, 2, RB, K), bf16),
            pltpu.VMEM((2, K, N), bf16),
            pltpu.VMEM((NC, R * RB, N), f32),
            pltpu.VMEM((NC, RB, N), f32),
            pltpu.VMEM((NC, RB, N), f32),
            pltpu.VMEM((NC, RB, N), f32),
            pltpu.VMEM((NC, RB, N), f32),
            pltpu.VMEM((NC, RB, N), bf16),
            dma((NC,)), dma((NC,)), dma((NC,)),
            dma((NP,)), dma((NP,)), dma((NP,)),
            dma((NC, R)), dma((NC, R)), dma((NC, R)),
            dma((NC, R)), dma((NC, R)), dma((NC, R)),
            dma((NC,)), dma((NC,)), dma((NC,)),
            dma((NC,)), dma((NC,)), dma((NC,)), dma((NC,)),
            dma((NC,)),
        ],
        compiler_params=pltpu.CompilerParams(
            collective_id=0, has_side_effects=True, vmem_limit_bytes=67043328),
    )(left_matrix, right_matrix)


def solution(mesh):
    shape = mesh.shape
    fits = shape["layer"] == 2 and shape["row"] == shape["col"] == 4
    local = functools.partial(fused, shape["row"]) if fits else plain
    in_specs = (P("row", ("layer", "col")), P(("layer", "row"), "col"))
    out_specs = P(("row", "layer"), "col")
    return jax.shard_map(local, mesh=mesh, in_specs=in_specs, out_specs=out_specs, check_vma=False)
```

time: 204 us -> 543 us (2.66)
  Pallas kernels: 201 us -> 541 us
    pallas_call x1, Pallas kernels: 201 us -> 541 us  [fused(): pl.pallas_call(functools.partial(kernel, R, NC, RB, TILE, NP), out_shape=...]
where the time goes in v1:
time: 543 us
  Pallas kernels  541 us (100%)
    pallas_call x1, Pallas kernels, fused(): pl.pallas_call(functools.partial(kernel, R, NC, RB, TILE, NP), out_shape=...  541 us

profile of v1, /device:TPU:0, one launch (start us, length us, event | category | flops | bytes accessed | tf_op | source)
XLA Modules:
  0.0 542.9 jit_solution(13763652149674349649)
XLA Ops:
  0.0 540.6 %shard_map.28 = bf16[256,2048]{1,0:T(8,128)(2,1)} custom-call(bf16[512,2048]{1,0:T(8,128)(2,1)} %a_hbm.1, bf16[2048,2048]{1,0:T(8,128)(2,1)} %b_hbm.1), custom_call_target="tpu_custom_call" | custom-call | tf_op jit(solution)/shard_map/pallas_call | solution.py:271
  540.6 2.3 copy.4

commit v2 on v1

v2 whole, which is shorter than its diff:
```python
import functools

import jax
import jax.numpy as jnp
from jax import lax
from jax.experimental import pallas as pl
from jax.experimental.pallas import tpu as pltpu
from jax.sharding import PartitionSpec as P

MESH = pl.DeviceIdType.MESH
PIECE_ROWS = 16
PARTS = 4
BSTEP = 1
AHEAD = 3
RIDE = 0
RELAY = 1
DEPART = 3
HOP = 1
LAG = 1
SETTLE = 2
FINISH = 2


def kernel(R, NU, RB, TN, a_hbm, b_hbm, o_hbm, abuf, tbuf, rbuf, bbuf, cbuf, dxin, dyin, sxin, syin, obuf,
           la, ls, lr, lb, bs, br, ar, us, ws, tr, tz, tx, rr, rs, cd, dxr, dyr, cx, cy, sxr, syr, lo):
    l = lax.axis_index("layer")
    i = lax.axis_index("row")
    z = lax.axis_index("col")
    x = lax.rem(i, 2)
    y = lax.div(i, 2)
    xn = 2 * y + 1 - x
    yn = 2 * (1 - y) + x
    dn = 2 * (1 - y) + 1 - x
    half = NU // 2 * RB
    GB = 2 * RB
    NP = bbuf.shape[2] // TN
    NV = NU // 4 * NP
    last = R - 1
    home = i == z

    def remote(src, dst, send, recv, **where):
        return pltpu.make_async_remote_copy(
            src_ref=src, dst_ref=dst, send_sem=send, recv_sem=recv,
            device_id=where, device_id_type=MESH)

    def apiece(u, m):
        return abuf.at[lax.div(u, 2), pl.ds(pl.multiple_of((2 * m + lax.rem(u, 2)) * RB, RB), RB)]

    def group(m):
        return pl.ds(pl.multiple_of(m * GB, GB), GB)

    def load(w, act_local, act_remote):
        u = 4 * lax.div(w, 2) + 2 * l + lax.rem(w, 2)
        mine = a_hbm.at[pl.ds(pl.multiple_of(l * half + w * RB, RB), RB)]
        other = a_hbm.at[pl.ds(pl.multiple_of((1 - l) * half + w * RB, RB), RB)]

        def place(spot):
            if act_local is not None:
                act_local(pltpu.make_async_copy(mine, spot, la.at[w]))
            if act_remote is not None:
                act_remote(remote(other, spot, ls, lr.at[w], layer=1 - l))

        @pl.when(home)
        def _():
            place(apiece(u, i))

        @pl.when(jnp.logical_not(home))
        def _():
            place(tbuf.at[u, z])

    def loaded(u):
        w = 2 * lax.div(u, 4) + lax.rem(u, 2)
        h = lax.rem(lax.div(u, 2), 2)

        @pl.when(h == l)
        def _():
            pltpu.make_async_copy(tbuf.at[u, z], tbuf.at[u, z], la.at[w]).wait()

        @pl.when(h != l)
        def _():
            remote(tbuf.at[u, z], tbuf.at[u, z], ls, lr.at[w], layer=1 - l).wait_recv()

    def part(p):
        return pl.ds(p * TN if isinstance(p, int) else pl.multiple_of(p * TN, TN), TN)

    def b_load(p):
        return pltpu.make_async_copy(b_hbm.at[:, part(p)], bbuf.at[l, :, part(p)], lb.at[p])

    def b_swap(p):
        return remote(b_hbm.at[:, part(p)], bbuf.at[l, :, part(p)], bs, br.at[p], layer=1 - l)

    def cross(u, k, act):
        @pl.when(k == dn)
        def _():
            act(remote(tbuf.at[u, k], rbuf.at[u], tx.at[k], rr.at[u], row=xn))

        @pl.when(k != dn)
        def _():
            act(remote(tbuf.at[u, k], apiece(u, i), tx.at[k], ar.at[u, i], row=k))

    def relay(u):
        return remote(rbuf.at[u], apiece(u, xn), rs, ar.at[u, xn], row=yn)

    relaying = (z == yn) | ((xn == last) & (yn < z)) | ((xn == 0) & (yn > z))

    def onward(u, k, act):
        for side, step in ((last, 1), (0, -1)):
            @pl.when((i == side) & (z != side))
            def _():
                act(remote(tbuf.at[u, k], tbuf.at[u, k], tz.at[k], tr.at[u, k], col=z + step))

    def passing(act):
        for d in range(1, R):
            for side, step in ((last, -1), (0, 1)):
                k = z + step * d

                @pl.when((i == side) & (k >= 0) & (k < R))
                def _():
                    act(k, d)

    def forward(u, m, act):
        @pl.when((m < last) & (i <= z) & (z < last))
        def _():
            act(remote(apiece(u, m), apiece(u, m), us.at[m], ar.at[u, m], col=z + 1))

        @pl.when((m > 0) & (i >= z) & (z > 0))
        def _():
            act(remote(apiece(u, m), apiece(u, m), ws.at[m], ar.at[u, m], col=z - 1))

    def arrived(u, m):
        return remote(apiece(u, m), apiece(u, m), us.at[m], ar.at[u, m], row=xn)

    def x_first(r):
        return (r == 1) | (r == 2) | ((r == 0) & (z == 2)) | ((r == 3) & (z == 1))

    here_x = x_first(i)
    side_x = x_first(xn)
    side_y = jnp.logical_not(x_first(yn))

    def far(v, act):
        @pl.when(here_x)
        def _():
            act(remote(cbuf.at[v, group(dn)], dxin.at[v], cd, dxr.at[v], row=xn))

        @pl.when(jnp.logical_not(here_x))
        def _():
            act(remote(cbuf.at[v, group(dn)], dyin.at[v], cd, dyr.at[v], row=yn))

    def to_x(v):
        return remote(cbuf.at[v, group(xn)], sxin.at[v], cx, sxr.at[v], row=xn)

    def to_y(v):
        return remote(cbuf.at[v, group(yn)], syin.at[v], cy, syr.at[v], row=yn)

    def out(v):
        return pltpu.make_async_copy(
            obuf.at[v], o_hbm.at[group(lax.div(v, NP)), part(lax.rem(v, NP))], lo)

    @pl.loop(0, NU // 2)
    def _(w):
        load(w, lambda t: t.start(), None)

    barrier = pltpu.get_barrier_semaphore()
    for where in ({"layer": 1 - l}, {"row": xn}, {"row": yn}, {"row": dn}):
        pl.semaphore_signal(barrier, inc=1, device_id=where, device_id_type=MESH)

    @pl.when(z > 0)
    def _():
        pl.semaphore_signal(barrier, inc=1, device_id={"col": z - 1}, device_id_type=MESH)

    @pl.when(z < last)
    def _():
        pl.semaphore_signal(barrier, inc=1, device_id={"col": z + 1}, device_id_type=MESH)

    pl.semaphore_wait(barrier, 4 + (z > 0).astype(jnp.int32) + (z < last).astype(jnp.int32))

    @pl.loop(0, NU // 2)
    def _(w):
        load(w, None, lambda t: t.start())

    def launch(u):
        loaded(u)

        @pl.when(jnp.logical_not(home))
        def _():
            cross(u, z, lambda t: t.start())

    def leave(u):
        @pl.when(jnp.logical_not(home))
        def _():
            onward(u, z, lambda t: t.start())

    def pass_on(s):
        def act(k, d):
            u = s - HOP * d

            @pl.when((u >= 0) & (u < NU))
            def _():
                remote(tbuf.at[u, k], tbuf.at[u, k], tz.at[k], tr.at[u, k], row=xn).wait_recv()
                onward(u, k, lambda t: t.start())
                cross(u, k, lambda t: t.start())
        passing(act)

    def hand_on(u):
        @pl.when(relaying)
        def _():
            remote(rbuf.at[u], rbuf.at[u], rs, rr.at[u], row=xn).wait_recv()
            relay(u).start()

    def depart(u):
        @pl.when(home)
        def _():
            forward(u, i, lambda t: t.start())

    def spread(u):
        for m in (i, xn, yn, dn):
            wanted = (home & (i != m)) | ((i < z) & (m < last)) | ((i > z) & (m > 0))

            @pl.when(wanted)
            def _():
                arrived(u, m).wait_recv()
                forward(u, m, lambda t: t.start())

    def multiply(v):
        g = lax.div(v, NP)
        p = lax.rem(v, NP)

        @pl.when(p == 0)
        def _():
            @pl.when(i < z)
            def _():
                for e in range(4):
                    arrived(4 * g + e, last).wait_recv()

            @pl.when(i > z)
            def _():
                for e in range(4):
                    arrived(4 * g + e, 0).wait_recv()

        cbuf[v] = (
            jnp.dot(abuf[2 * g], bbuf[0, :, part(p)], preferred_element_type=jnp.float32)
            + jnp.dot(abuf[2 * g + 1], bbuf[1, :, part(p)], preferred_element_type=jnp.float32))
        far(v, lambda t: t.start())

    def settle(v):
        @pl.when(side_y)
        def _():
            remote(dyin.at[v], dyin.at[v], cd, dyr.at[v], row=yn).wait_recv()
            cbuf[v, group(xn)] = cbuf[v, group(xn)] + dyin[v]
        to_x(v).start()

        @pl.when(side_x)
        def _():
            remote(dxin.at[v], dxin.at[v], cd, dxr.at[v], row=xn).wait_recv()
            cbuf[v, group(yn)] = cbuf[v, group(yn)] + dxin[v]
        to_y(v).start()

    def finish(v):
        to_x(v).wait_recv()
        to_y(v).wait_recv()
        obuf[v] = (cbuf[v, group(i)] + sxin[v] + syin[v]).astype(jnp.bfloat16)
        out(v).start()

    away = HOP * jnp.abs(z - i)
    ML = 3 + LAG
    RL = RELAY + jnp.where(z == yn, -AHEAD, HOP * jnp.abs(z - yn))
    SL = HOP * last + ML + SETTLE
    FL = SL + FINISH

    @pl.loop(-AHEAD, NU + FL)
    def _(s):
        def at(lag, total, act):
            c = s - lag

            @pl.when((c >= 0) & (c < total))
            def _():
                act(c)

        for p in range(NP):
            @pl.when(s == BSTEP)
            def _():
                b_load(p).start()
                b_swap(p).start()

        at(-AHEAD, NU, launch)
        at(-RIDE, NU, leave)
        at(-DEPART, NU, depart)
        at(RL, NU, hand_on)
        pass_on(s)
        at(away, NU, spread)

        for p in range(NP):
            @pl.when(s == away + ML + p)
            def _():
                b_load(p).wait()
                b_swap(p).wait_recv()

        at(away + ML, NV, multiply)
        at(SL, NV, settle)
        at(FL, NV, finish)

    def sent(ref, sem):
        remote(ref, ref, sem, rr.at[0], row=xn).wait_send()

    def sent_on(k):
        sent(tbuf.at[:, k], tx.at[k])

        @pl.when(((i == last) & (z != last)) | ((i == 0) & (z != 0)))
        def _():
            sent(tbuf.at[:, k], tz.at[k])

    @pl.when(jnp.logical_not(home))
    def _():
        sent_on(z)

    passing(lambda k, d: sent_on(k))

    for m in range(R):
        @pl.when((m < last) & (i <= z) & (z < last))
        def _():
            sent(tbuf.at[:, m], us.at[m])

        @pl.when((m > 0) & (i >= z) & (z > 0))
        def _():
            sent(tbuf.at[:, m], ws.at[m])

    @pl.when(relaying)
    def _():
        sent(rbuf, rs)

    sent(tbuf.at[pl.ds(0, NU // 2), 0], ls)
    sent(bbuf.at[l], bs)
    sent(dxin, cd)
    sent(sxin, cx)
    sent(syin, cy)
    pltpu.make_async_copy(obuf, obuf, lo).wait()


def plain(left_matrix, right_matrix):
    left_rows = lax.all_gather(left_matrix, "col", axis=1, tiled=True)
    right_joined = lax.all_gather(right_matrix, "row", axis=0, tiled=True)
    summed = lax.psum_scatter(
        jnp.dot(left_rows, right_joined, preferred_element_type=jnp.float32),
        "layer",
        scatter_dimension=0,
        tiled=True,
    )
    return summed.astype(jnp.bfloat16)


def fused(R, left_matrix, right_matrix):
    rows, K = left_matrix.shape
    N = right_matrix.shape[1]
    half, RB, NP = rows // 2, PIECE_ROWS, PARTS
    NU, TN, GB = 2 * half // RB, N // NP, 2 * RB
    NV = NU // 4 * NP
    bf16, f32 = jnp.bfloat16, jnp.float32
    dma = pltpu.SemaphoreType.DMA
    return pl.pallas_call(
        functools.partial(kernel, R, NU, RB, TN),
        out_shape=jax.ShapeDtypeStruct((half, N), bf16),
        in_specs=[pl.BlockSpec(memory_space=pl.ANY)] * 2,
        out_specs=pl.BlockSpec(memory_space=pl.ANY),
        scratch_shapes=[
            pltpu.VMEM((NU // 2, R * GB, K), bf16),
            pltpu.VMEM((NU, R, RB, K), bf16),
            pltpu.VMEM((NU, RB, K), bf16),
            pltpu.VMEM((2, K, N), bf16),
            pltpu.VMEM((NV, R * GB, TN), f32),
            pltpu.VMEM((NV, GB, TN), f32),
            pltpu.VMEM((NV, GB, TN), f32),
            pltpu.VMEM((NV, GB, TN), f32),
            pltpu.VMEM((NV, GB, TN), f32),
            pltpu.VMEM((NV, GB, TN), bf16),
            dma((NU // 2,)), dma, dma((NU // 2,)),
            dma((NP,)), dma, dma((NP,)),
            dma((NU, R)), dma((R,)), dma((R,)),
            dma((NU, R)), dma((R,)), dma((R,)),
            dma((NU,)), dma,
            dma, dma((NV,)), dma((NV,)),
            dma, dma, dma((NV,)), dma((NV,)),
            dma,
        ],
        compiler_params=pltpu.CompilerParams(
            collective_id=0, has_side_effects=True, vmem_limit_bytes=67043328),
    )(left_matrix, right_matrix)


def solution(mesh):
    shape = mesh.shape
    fits = shape["layer"] == 2 and shape["row"] == shape["col"] == 4
    local = functools.partial(fused, shape["row"]) if fits else plain
    in_specs = (P("row", ("layer", "col")), P(("layer", "row"), "col"))
    out_specs = P(("row", "layer"), "col")
    return jax.shard_map(local, mesh=mesh, in_specs=in_specs, out_specs=out_specs, check_vma=False)
```

time: 543 us -> 184 us (0.34)
  Pallas kernels: 541 us -> 181 us
    pallas_call x1, Pallas kernels: 541 us -> 181 us  [fused(): pl.pallas_call(functools.partial(kernel, R, NU, RB, TN), out_shape=jax.Sh...]
where the time goes in v2:
time: 184 us; the launch traced here: 183 us
  Pallas kernels  181 us (98%)
  local copies, waits for them, and re-layouts  2.3 us (1%)
    pallas_call x1, Pallas kernels, fused(): pl.pallas_call(functools.partial(kernel, R, NU, RB, TN), out_shape=jax.Sh...  181 us

profile of v2, /device:TPU:0, one launch (start us, length us, event | category | flops | bytes accessed | tf_op | source)
XLA Modules:
  0.0 183.4 jit_solution(17246983695689660232)
XLA Ops:
  0.0 181.1 %shard_map.28 = bf16[256,2048]{1,0:T(8,128)(2,1)} custom-call(bf16[512,2048]{1,0:T(8,128)(2,1)} %a_hbm.1, bf16[2048,2048]{1,0:T(8,128)(2,1)} %b_hbm.1), custom_call_target="tpu_custom_call" | custom-call | tf_op jit(solution)/shard_map/pallas_call | solution.py:359
  181.1 2.3 %copy.4 = bf16[256,2048]{1,0:T(8,128)(2,1)} copy(bf16[256,2048]{1,0:T(8,128)(2,1)} %shard_map.28) | data formatting | bytes 2097152

commit v3 on v2

--- a/solution.py
+++ b/solution.py
@@ -9,20 +9,20 @@
 
 MESH = pl.DeviceIdType.MESH
 PIECE_ROWS = 16
-PARTS = 4
+PARTS = 2
 BSTEP = 1
 AHEAD = 3
-RIDE = 0
+RIDE = 2
 RELAY = 1
-DEPART = 3
+DEPART = 2
 HOP = 1
 LAG = 1
 SETTLE = 2
-FINISH = 2
-
-
-def kernel(R, NU, RB, TN, a_hbm, b_hbm, o_hbm, abuf, tbuf, rbuf, bbuf, cbuf, dxin, dyin, sxin, syin, obuf,
-           la, ls, lr, lb, bs, br, ar, us, ws, tr, tz, tx, rr, rs, cd, dxr, dyr, cx, cy, sxr, syr, lo):
+FINISH = 4
+
+
+def kernel(R, NU, RB, TN, a_hbm, b_hbm, o_hbm, abuf, tbuf, rbuf, bbuf, cbuf, dxin, dyin, sums, obuf,
+           la, ls, lr, lb, bs, br, ar, us, ws, tr, tz, tx, rr, rs, cd, dxr, dyr, cx, cy, sr, lo):
     l = lax.axis_index("layer")
     i = lax.axis_index("row")
     z = lax.axis_index("col")
@@ -32,9 +32,8 @@
     yn = 2 * (1 - y) + x
     dn = 2 * (1 - y) + 1 - x
     half = NU // 2 * RB
-    GB = 2 * RB
     NP = bbuf.shape[2] // TN
-    NV = NU // 4 * NP
+    NV = NU // 2 * NP
     last = R - 1
     home = i == z
 
@@ -44,13 +43,13 @@
             device_id=where, device_id_type=MESH)
 
     def apiece(u, m):
-        return abuf.at[lax.div(u, 2), pl.ds(pl.multiple_of((2 * m + lax.rem(u, 2)) * RB, RB), RB)]
+        return abuf.at[u, group(m)]
 
     def group(m):
-        return pl.ds(pl.multiple_of(m * GB, GB), GB)
+        return pl.ds(pl.multiple_of(m * RB, RB), RB)
 
     def load(w, act_local, act_remote):
-        u = 4 * lax.div(w, 2) + 2 * l + lax.rem(w, 2)
+        u = 2 * w + l
         mine = a_hbm.at[pl.ds(pl.multiple_of(l * half + w * RB, RB), RB)]
         other = a_hbm.at[pl.ds(pl.multiple_of((1 - l) * half + w * RB, RB), RB)]
 
@@ -69,8 +68,8 @@
             place(tbuf.at[u, z])
 
     def loaded(u):
-        w = 2 * lax.div(u, 4) + lax.rem(u, 2)
-        h = lax.rem(lax.div(u, 2), 2)
+        w = lax.div(u, 2)
+        h = lax.rem(u, 2)
 
         @pl.when(h == l)
         def _():
@@ -107,7 +106,7 @@
         for side, step in ((last, 1), (0, -1)):
             @pl.when((i == side) & (z != side))
             def _():
-                act(remote(tbuf.at[u, k], tbuf.at[u, k], tz.at[k], tr.at[u, k], col=z + step))
+                act(remote(tbuf.at[u, k], tbuf.at[u, k], tz.at[k], tr.at[u, jnp.abs(k - z)], col=z + step))
 
     def passing(act):
         for d in range(1, R):
@@ -147,10 +146,10 @@
             act(remote(cbuf.at[v, group(dn)], dyin.at[v], cd, dyr.at[v], row=yn))
 
     def to_x(v):
-        return remote(cbuf.at[v, group(xn)], sxin.at[v], cx, sxr.at[v], row=xn)
+        return remote(cbuf.at[v, group(xn)], sums.at[v, 0], cx, sr.at[v], row=xn)
 
     def to_y(v):
-        return remote(cbuf.at[v, group(yn)], syin.at[v], cy, syr.at[v], row=yn)
+        return remote(cbuf.at[v, group(yn)], sums.at[v, 1], cy, sr.at[v], row=yn)
 
     def out(v):
         return pltpu.make_async_copy(
@@ -192,11 +191,11 @@
 
     def pass_on(s):
         def act(k, d):
-            u = s - HOP * d
+            u = s - HOP * d + RIDE
 
             @pl.when((u >= 0) & (u < NU))
             def _():
-                remote(tbuf.at[u, k], tbuf.at[u, k], tz.at[k], tr.at[u, k], row=xn).wait_recv()
+                remote(tbuf.at[u, k], tbuf.at[u, k], tz.at[k], tr.at[u, d - 1], row=xn).wait_recv()
                 onward(u, k, lambda t: t.start())
                 cross(u, k, lambda t: t.start())
         passing(act)
@@ -208,13 +207,15 @@
             relay(u).start()
 
     def depart(u):
-        @pl.when(home)
-        def _():
-            forward(u, i, lambda t: t.start())
+        @pl.when(jnp.logical_not(home))
+        def _():
+            arrived(u, i).wait_recv()
+
+        forward(u, i, lambda t: t.start())
 
     def spread(u):
-        for m in (i, xn, yn, dn):
-            wanted = (home & (i != m)) | ((i < z) & (m < last)) | ((i > z) & (m > 0))
+        for m in (xn, yn, dn):
+            wanted = home | ((i < z) & (m < last)) | ((i > z) & (m > 0))
 
             @pl.when(wanted)
             def _():
@@ -229,45 +230,62 @@
         def _():
             @pl.when(i < z)
             def _():
-                for e in range(4):
-                    arrived(4 * g + e, last).wait_recv()
+                for e in range(2):
+                    arrived(2 * g + e, last).wait_recv()
 
             @pl.when(i > z)
             def _():
-                for e in range(4):
-                    arrived(4 * g + e, 0).wait_recv()
-
-        cbuf[v] = (
-            jnp.dot(abuf[2 * g], bbuf[0, :, part(p)], preferred_element_type=jnp.float32)
-            + jnp.dot(abuf[2 * g + 1], bbuf[1, :, part(p)], preferred_element_type=jnp.float32))
+                for e in range(2):
+                    arrived(2 * g + e, 0).wait_recv()
+
+        dots(v, 0)
+
+    def dots(v, e):
+        g = lax.div(v, NP)
+        width = TN // 2
+        columns = pl.ds(pl.multiple_of(lax.rem(v, NP) * TN + e * width, width), width)
+        cbuf[v, :, e * width:(e + 1) * width] = (
+            jnp.dot(abuf[2 * g], bbuf[0, :, columns], preferred_element_type=jnp.float32)
+            + jnp.dot(abuf[2 * g + 1], bbuf[1, :, columns], preferred_element_type=jnp.float32))
+
+    def partials(v):
+        dots(v, 1)
         far(v, lambda t: t.start())
 
-    def settle(v):
+        @pl.when(jnp.logical_not(side_y))
+        def _():
+            to_x(v).start()
+
+        @pl.when(jnp.logical_not(side_x))
+        def _():
+            to_y(v).start()
+
+    def settle_x(v):
         @pl.when(side_y)
         def _():
             remote(dyin.at[v], dyin.at[v], cd, dyr.at[v], row=yn).wait_recv()
             cbuf[v, group(xn)] = cbuf[v, group(xn)] + dyin[v]
-        to_x(v).start()
-
+            to_x(v).start()
+
+    def settle_y(v):
         @pl.when(side_x)
         def _():
             remote(dxin.at[v], dxin.at[v], cd, dxr.at[v], row=xn).wait_recv()
             cbuf[v, group(yn)] = cbuf[v, group(yn)] + dxin[v]
-        to_y(v).start()
+            to_y(v).start()
 
     def finish(v):
-        to_x(v).wait_recv()
-        to_y(v).wait_recv()
-        obuf[v] = (cbuf[v, group(i)] + sxin[v] + syin[v]).astype(jnp.bfloat16)
+        remote(sums.at[v], sums.at[v], cx, sr.at[v], row=xn).wait_recv()
+        obuf[v] = (cbuf[v, group(i)] + sums[v, 0] + sums[v, 1]).astype(jnp.bfloat16)
         out(v).start()
 
     away = HOP * jnp.abs(z - i)
-    ML = 3 + LAG
-    RL = RELAY + jnp.where(z == yn, -AHEAD, HOP * jnp.abs(z - yn))
-    SL = HOP * last + ML + SETTLE
+    ML = 1 + LAG
+    RL = RELAY + jnp.where(z == yn, -AHEAD, HOP * jnp.abs(z - yn) - RIDE)
+    SL = HOP * last + ML + 1 + SETTLE
     FL = SL + FINISH
 
-    @pl.loop(-AHEAD, NU + FL)
+    @pl.loop(-max(AHEAD, RIDE, DEPART), NU + FL)
     def _(s):
         def at(lag, total, act):
             c = s - lag
@@ -284,9 +302,10 @@
 
         at(-AHEAD, NU, launch)
         at(-RIDE, NU, leave)
-        at(-DEPART, NU, depart)
+        at(away - DEPART, NU, depart)
         at(RL, NU, hand_on)
         pass_on(s)
+        at(away + ML + 1, NV, partials)
         at(away, NU, spread)
 
         for p in range(NP):
@@ -296,7 +315,8 @@
                 b_swap(p).wait_recv()
 
         at(away + ML, NV, multiply)
-        at(SL, NV, settle)
+        at(ML + 1 + SETTLE + jnp.maximum(away, HOP * jnp.abs(z - yn)), NV, settle_x)
+        at(ML + 1 + SETTLE + jnp.maximum(away, HOP * jnp.abs(z - xn)), NV, settle_y)
         at(FL, NV, finish)
 
     def sent(ref, sem):
@@ -331,8 +351,8 @@
     sent(tbuf.at[pl.ds(0, NU // 2), 0], ls)
     sent(bbuf.at[l], bs)
     sent(dxin, cd)
-    sent(sxin, cx)
-    sent(syin, cy)
+    sent(dxin, cx)
+    sent(dxin, cy)
     pltpu.make_async_copy(obuf, obuf, lo).wait()
 
 
@@ -352,8 +372,8 @@
     rows, K = left_matrix.shape
     N = right_matrix.shape[1]
     half, RB, NP = rows // 2, PIECE_ROWS, PARTS
-    NU, TN, GB = 2 * half // RB, N // NP, 2 * RB
-    NV = NU // 4 * NP
+    NU, TN, GB = 2 * half // RB, N // NP, RB
+    NV = NU // 2 * NP
     bf16, f32 = jnp.bfloat16, jnp.float32
     dma = pltpu.SemaphoreType.DMA
     return pl.pallas_call(
@@ -362,23 +382,22 @@
         in_specs=[pl.BlockSpec(memory_space=pl.ANY)] * 2,
         out_specs=pl.BlockSpec(memory_space=pl.ANY),
         scratch_shapes=[
-            pltpu.VMEM((NU // 2, R * GB, K), bf16),
+            pltpu.VMEM((NU, R * RB, K), bf16),
             pltpu.VMEM((NU, R, RB, K), bf16),
             pltpu.VMEM((NU, RB, K), bf16),
             pltpu.VMEM((2, K, N), bf16),
             pltpu.VMEM((NV, R * GB, TN), f32),
             pltpu.VMEM((NV, GB, TN), f32),
             pltpu.VMEM((NV, GB, TN), f32),
-            pltpu.VMEM((NV, GB, TN), f32),
-            pltpu.VMEM((NV, GB, TN), f32),
+            pltpu.VMEM((NV, 2, GB, TN), f32),
             pltpu.VMEM((NV, GB, TN), bf16),
             dma((NU // 2,)), dma, dma((NU // 2,)),
             dma((NP,)), dma, dma((NP,)),
             dma((NU, R)), dma((R,)), dma((R,)),
-            dma((NU, R)), dma((R,)), dma((R,)),
+            dma((NU, R - 1)), dma((R,)), dma((R,)),
             dma((NU,)), dma,
             dma, dma((NV,)), dma((NV,)),
-            dma, dma, dma((NV,)), dma((NV,)),
+            dma, dma, dma((NV,)),
             dma,
         ],
         compiler_params=pltpu.CompilerParams(

time: 184 us -> 177 us (0.962)
  Pallas kernels: 181 us -> 175 us
    pallas_call x1, Pallas kernels: 181 us -> 175 us  [fused(): pl.pallas_call(functools.partial(kernel, R, NU, RB, TN), out_shape=jax.Sh...]
where the time goes in v3:
time: 177 us
  Pallas kernels  175 us (99%)
  local copies, waits for them, and re-layouts  2.3 us (1%)
    pallas_call x1, Pallas kernels, fused(): pl.pallas_call(functools.partial(kernel, R, NU, RB, TN), out_shape=jax.Sh...  175 us

profile of v3, /device:TPU:0, one launch (start us, length us, event | category | flops | bytes accessed | tf_op | source)
XLA Modules:
  0.0 177.3 jit_solution(16476141258071904140)
XLA Ops:
  0.0 175.0 %shard_map.28 = bf16[256,2048]{1,0:T(8,128)(2,1)} custom-call(bf16[512,2048]{1,0:T(8,128)(2,1)} %a_hbm.1, bf16[2048,2048]{1,0:T(8,128)(2,1)} %b_hbm.1), custom_call_target="tpu_custom_call" | custom-call | tf_op jit(solution)/shard_map/pallas_call | solution.py:379
  175.0 2.3 %copy.4 = bf16[256,2048]{1,0:T(8,128)(2,1)} copy(bf16[256,2048]{1,0:T(8,128)(2,1)} %shard_map.28) | data formatting | bytes 2097152

commit v4 on v3

--- a/solution.py
+++ b/solution.py
@@ -11,7 +11,7 @@
 PIECE_ROWS = 16
 PARTS = 2
 BSTEP = 1
-AHEAD = 3
+AHEAD = 2
 RIDE = 2
 RELAY = 1
 DEPART = 2

time: 177 us -> 177 us (level)
  no operation moved by 1% of the time
where the time goes in v4:
time: 177 us; the launch traced here: 176 us
  Pallas kernels  174 us (98%)
  local copies, waits for them, and re-layouts  2.3 us (1%)
    pallas_call x1, Pallas kernels, fused(): pl.pallas_call(functools.partial(kernel, R, NU, RB, TN), out_shape=jax.Sh...  174 us

profile of v4, /device:TPU:0, one launch (start us, length us, event | category | flops | bytes accessed | tf_op | source)
XLA Modules:
  0.0 176.4 jit_solution(10200537895617810309)
XLA Ops:
  0.0 174.1 %shard_map.28 = bf16[256,2048]{1,0:T(8,128)(2,1)} custom-call(bf16[512,2048]{1,0:T(8,128)(2,1)} %a_hbm.1, bf16[2048,2048]{1,0:T(8,128)(2,1)} %b_hbm.1), custom_call_target="tpu_custom_call" | custom-call | tf_op jit(solution)/shard_map/pallas_call | solution.py:379
  174.1 2.3 %copy.4 = bf16[256,2048]{1,0:T(8,128)(2,1)} copy(bf16[256,2048]{1,0:T(8,128)(2,1)} %shard_map.28) | data formatting | bytes 2097152
